TPU v7x, 512 devices: a 4x2x32 block of a 4x8x32 slice. The times are simulated.
512 devices in a mesh: groups: 2 (over y), fsdp: 32 (over z), tensor: 8 (over x, core).
Axes of the slice: x: 4, y: 2, z: 32, core: 2. Of those that a mesh axis runs over, the one named last changes fastest.
The devices are a block of a 4x8x32 slice.
Arguments:
- tokens: bfloat16 [16384, 4608], P(('groups', 'fsdp'), 'tensor'), parts along dimension 0, may hold values from -100 to 100
- norm_gain: bfloat16 [4608], P('tensor'), may hold values from 0.25 to 1.75
- w_query: bfloat16 [4608, 4096], P('fsdp', 'tensor'), may hold values from -0.5 to 0.5
- w_key: bfloat16 [4608, 2048], P('fsdp', 'tensor'), may hold values from -0.09375 to 0.09375
- w_value: bfloat16 [4608, 2048], P('fsdp', 'tensor'), may hold values from -0.09375 to 0.09375
- w_out: bfloat16 [4096, 4608], P('tensor', 'fsdp'), may hold values from -0.5 to 0.5
- post_gain: bfloat16 [4608], P('tensor'), may hold values from 0.25 to 1.75
Outputs:
- mixed: float32 [16384, 4608], P(('groups', 'fsdp'), 'tensor'), parts along dimension 0
There are 2 independent parts, one for each index of `groups`. A program takes and returns all parts, laid end to end along the dimension named above; an argument that names none is the same for every part. Nothing has to cross between parts.
All inputs are finite; a program needn't handle non-finite values.
Results may differ from a plain program's by a relative error of at most 0.0053.
Values may be sent and summed in bfloat16 or wider, within the bound.
A program may use at most 128 MiB of HBM per device.

v0:
```python
import jax
import jax.numpy as jnp
from jax import lax
from jax.sharding import PartitionSpec as P

D = 4608
HEAD_DIM = 128
eps_norm = 1e-06
soft_cap = 50.0
attn_scale = 144.0 ** (-0.5)
rope_base = 10000.0


def copy_for_each(array, axis):
    count = lax.axis_size(axis)
    return lax.all_to_all(
        jnp.broadcast_to(array[None], (count, *array.shape)), axis, 0, 0, tiled=True
    )


def of_everyone(array, axis):
    return copy_for_each(array, axis).sum(axis=0)


def joined_along(pieces, dim):
    pieces = jnp.moveaxis(pieces, 0, dim)
    lengths = pieces.shape
    return pieces.reshape(*lengths[:dim], lengths[dim] * lengths[dim + 1], *lengths[dim + 2 :])


def gather_directly(array, axis, dim):
    return joined_along(copy_for_each(array, axis), dim)


def side_by_side(arrays, axis, dim, along):
    ends, at = ([], 0)
    for a in arrays[:-1]:
        at += a.shape[along]
        ends.append(at)
    both = jnp.concatenate(arrays, axis=along)
    return tuple(jnp.split(lax.all_gather(both, axis, axis=dim, tiled=True), ends, axis=along))


def in_blocks(array, dim, count):
    before, after = (array.shape[:dim], array.shape[dim + 1 :])
    return jnp.moveaxis(array.reshape(*before, count, -1, *after), dim, 0)


def summed_on_arrival(array, axis, dim):
    count = lax.axis_size(axis)
    pieces = lax.all_to_all(in_blocks(array, dim, count), axis, 0, 0, tiled=True)
    return jnp.sum(pieces.astype(jnp.float32), axis=0)


def rotate(values, position):
    head_dim = values.shape[-1]
    half = head_dim // 2
    freq = rope_base ** (-(jnp.arange(half, dtype=jnp.float32) * 2.0 / head_dim))
    angle = position.astype(jnp.float32)[:, None] * freq[None, :]
    cosine = jnp.cos(angle)[:, None, :]
    sine = jnp.sin(angle)[:, None, :]
    first = values[..., :half]
    second = values[..., half:]
    return jnp.concatenate(
        [first * cosine - second * sine, second * cosine + first * sine], axis=-1
    )


def attend(query, keys, values, position):
    count, heads, head_dim = query.shape
    kv_count = keys.shape[1]
    grouped = query.reshape(count, kv_count, heads // kv_count, head_dim)
    scores = (
        jnp.einsum("nkgd,mkd->kgnm", grouped, keys, preferred_element_type=jnp.float32) * attn_scale
    )
    capped = soft_cap * jnp.tanh(scores / soft_cap)
    allowed = position[None, :] <= position[:, None]
    weights = jnp.where(allowed, jnp.exp(capped), 0.0)
    probs = (weights / jnp.sum(weights, axis=-1, keepdims=True)).astype(jnp.bfloat16)
    mixed = jnp.einsum("kgnm,mkd->nkgd", probs, values, preferred_element_type=jnp.float32)
    return mixed.reshape(count, heads * head_dim).astype(jnp.bfloat16)


def on_device(tokens, norm_gain, w_query, w_key, w_value, w_out, post_gain):
    rows = tokens.shape[0]
    local = tokens.astype(jnp.float32)
    total = of_everyone(jnp.sum(local * local, axis=1), "tensor")
    normed = (
        local * lax.rsqrt(total / D + eps_norm)[:, None] * norm_gain.astype(jnp.float32)
    ).astype(jnp.bfloat16)
    whole = gather_directly(normed, "tensor", 1)
    pieces = side_by_side((w_query, w_key, w_value), "fsdp", 0, 1)
    query_raw, key_raw, value_raw = tuple(
        (jnp.dot(whole, piece, preferred_element_type=jnp.float32) for piece in pieces)
    )
    position = jnp.arange(rows, dtype=jnp.int32)
    local_heads = w_query.shape[1] // HEAD_DIM
    local_kv = w_key.shape[1] // HEAD_DIM
    query = rotate(query_raw.reshape(rows, local_heads, HEAD_DIM), position).astype(jnp.bfloat16)
    key = rotate(key_raw.reshape(rows, local_kv, HEAD_DIM), position).astype(jnp.bfloat16)
    value = value_raw.astype(jnp.bfloat16).reshape(rows, local_kv, HEAD_DIM)
    attn = attend(query, key, value, position)
    partial_value = jnp.dot(
        attn, lax.all_gather(w_out, "fsdp", axis=1, tiled=True), preferred_element_type=jnp.float32
    )
    proj = summed_on_arrival(partial_value.astype(jnp.bfloat16), "tensor", 1)
    post_total = of_everyone(jnp.sum(proj * proj, axis=1), "tensor")
    branch = proj * lax.rsqrt(post_total / D + eps_norm)[:, None] * post_gain.astype(jnp.float32)
    return tokens.astype(jnp.float32) + branch


def solution(mesh):
    placed = (
        P(("groups", "fsdp"), "tensor"),
        P("tensor"),
        P("fsdp", "tensor"),
        P("fsdp", "tensor"),
        P("fsdp", "tensor"),
        P("tensor", "fsdp"),
        P("tensor"),
    )
    return jax.shard_map(
        on_device,
        mesh=mesh,
        in_specs=placed,
        out_specs=P(("groups", "fsdp"), "tensor"),
        check_vma=False,
    )
```

profile of v0, /device:TPU:33, one launch (start us, length us, event | category | flops | bytes accessed | tf_op | source)
XLA Modules:
  0.0 380.2 jit_solution(6759158152972305025)
XLA Ops:
  6.5 0.0 all-gather.3.cloned.1.call-start
  6.6 1.7 pad_maximum_fusion
  8.3 0.1 all-gather.3.cloned.1.call-update
  8.3 0.1 all-gather.5.cloned.1.call-start
  8.4 0.7 all-gather.5.cloned.1.call-update
  9.2 1.1 fusion.10
  10.2 0.6 broadcast_in_dim.12
  10.8 44.7 %all-to-all-start = ((f32[8,1,256]{2,1,0:T(1,128)}), f32[8,1,256]{2,1,0:T(1,128)S(1)}, u32[]{:S(2)}, u32[]{:S(2)}) async-start(f32[8,1,256]{2,1,0:T(1,128)} %broadcast_in_dim.12), calls=%async_computation | async-start | bytes 16384 | tf_op jit(solution)/shard_map/all_to_all | solution.py:16
  55.5 0.7 convert_element_type.60
  56.2 4.0 %all-to-all-done = f32[8,1,256]{2,1,0:T(1,128)S(1)} async-done(((f32[8,1,256]{2,1,0:T(1,128)}), f32[8,1,256]{2,1,0:T(1,128)S(1)}, u32[]{:S(2)}, u32[]{:S(2)}) %all-to-all-start) | async-done | bytes 8224 | tf_op jit(solution)/shard_map/all_to_all | solution.py:16
  60.2 1.1 fusion.12
  61.3 1.6 broadcast_in_dim.13
  63.0 4.2 %all-to-all-start.1 = ((bf16[8,256,576]{1,2,0:T(8,128)(2,1)}), bf16[8,256,576]{1,2,0:T(8,128)(2,1)S(1)}, u32[]{:S(2)}, u32[]{:S(2)}) async-start(bf16[8,256,576]{1,2,0:T(8,128)(2,1)} %broadcast_in_dim.13), calls=%async_computation.1 | async-start | bytes 4718592 | tf_op jit(solution)/shard_map/all_to_all | solution.py:16
  67.2 0.3 multiply_cosine_fusion
  67.5 102.3 %all-gather.3.cloned.1.call-done = bf16[4608,1024]{1,0:T(8,128)(2,1)} async-done(((bf16[144,1024]{1,0:T(8,128)(2,1)}), bf16[4608,1024]{1,0:T(8,128)(2,1)}) %all-gather.3.cloned.1.call-update) | async-done | bytes 9437200 | tf_op jit(solution)/shard_map/all_gather | solution.py:41
  169.8 4.8 %slice_bitcast_fusion = bf16[512,4608]{0,1:T(8,128)(2,1)} fusion(bf16[4608,1024]{1,0:T(8,128)(2,1)} %all-gather.3.cloned.1.call-done), kind=kLoop, calls=%fused_computation.1 | loop fusion | bytes 9437184 | tf_op jit(solution)/shard_map/dot_general | solution.py:94
  174.6 6.8 %copy.36 = bf16[512,4608]{1,0:T(8,128)(2,1)} copy(bf16[512,4608]{0,1:T(8,128)(2,1)} %slice_bitcast_fusion) | data formatting | bytes 9437184 | tf_op jit(solution)/shard_map/dot_general | solution.py:94
  181.4 0.0 all-to-all-done.1
  181.4 0.0 copy-start.1
  181.4 4.6 %fusion.22 = f32[256,4,128]{0,2,1:T(8,128)S(1)} fusion(bf16[256,4608,1]{0,1,2:T(8,128)(2,1)S(1)} %bitcast.45, bf16[4,128,4608]{2,1,0:T(8,128)(2,1)} %bitcast.44), kind=kOutput, calls=%fused_computation.44 | convolution fusion | flops 1207959552 | bytes 7602176 | tf_op jit(solution)/shard_map/dot_general | solution.py:94
  186.0 0.0 copy-done.1
  186.0 0.1 subtract_convert_fusion
  186.1 0.2 copy.38
  186.2 0.2 copy.39
  186.4 1.8 slice_bitcast_fusion.1
  188.2 2.6 copy.34
  190.8 3.1 fusion.21
  193.9 0.0 copy-start.2
  194.0 0.6 fusion.6
  194.6 1.1 copy-done.2
  195.6 2.8 fusion.7
  198.4 0.3 convolution_convert_fusion.1
  198.7 103.8 %all-gather.5.cloned.1.call-done = bf16[512,4608]{0,1:T(8,128)(2,1)} async-done(((bf16[512,144]{0,1:T(8,128)(2,1)}), bf16[512,4608]{0,1:T(8,128)(2,1)}) %all-gather.5.cloned.1.call-update) | async-done | bytes 4718608 | tf_op jit(solution)/shard_map/all_gather | solution.py:104
  302.5 3.8 convolution_convert_fusion
  306.3 2.5 copy.42
  308.7 53.6 %all_to_all.22 = bf16[8,256,576]{1,2,0:T(8,128)(2,1)S(1)} all-to-all(bf16[8,256,576]{1,2,0:T(8,128)(2,1)} %bitcast.43), channel_id=1, replica_groups=mesh['groups'=2,'fsdp'=32,'tensor'=8] {'tensor'}, dimensions={0} | all-to-all | bytes 4718592 | tf_op jit(solution)/shard_map/all_to_all | solution.py:51
  362.3 0.0 copy-start.3
  362.3 0.0 copy-start
  362.3 0.3 convert_reduce_fusion
  362.6 0.1 multiply_reduce_fusion
  362.7 0.6 broadcast_in_dim.16
  363.3 4.3 %all-to-all-start.3 = ((f32[8,1,256]{2,1,0:T(1,128)}), f32[8,1,256]{2,1,0:T(1,128)S(1)}, u32[]{:S(2)}, u32[]{:S(2)}) async-start(f32[8,1,256]{2,1,0:T(1,128)} %broadcast_in_dim.16), calls=%async_computation.3 | async-start | bytes 16384 | tf_op jit(solution)/shard_map/all_to_all | solution.py:16
  367.6 0.0 copy-done.3
  367.6 4.7 %all-to-all-done.3 = f32[8,1,256]{2,1,0:T(1,128)S(1)} async-done(((f32[8,1,256]{2,1,0:T(1,128)}), f32[8,1,256]{2,1,0:T(1,128)S(1)}, u32[]{:S(2)}, u32[]{:S(2)}) %all-to-all-start.3) | async-done | bytes 8224 | tf_op jit(solution)/shard_map/all_to_all | solution.py:16
  372.4 0.0 copy-done
  372.4 1.0 convert_add_fusion
  (9 shorter events, 0.2 us)
Async XLA Ops:
  6.5 163.2 %all-gather.3.cloned.1.call-start = ((), (), s32[]{:S(2)}) async-start(), calls=%async_computation.4 | async-start | bytes 9732096 | tf_op jit(solution)/shard_map/all_gather | solution.py:41
  8.3 294.2 %all-gather.5.cloned.1.call-start = ((), (), s32[]{:S(2)}) async-start(), calls=%async_computation.5 | async-start | bytes 4866048 | tf_op jit(solution)/shard_map/all_gather | solution.py:104
  10.8 49.4 %all-to-all-start = ((f32[8,1,256]{2,1,0:T(1,128)}), f32[8,1,256]{2,1,0:T(1,128)S(1)}, u32[]{:S(2)}, u32[]{:S(2)}) async-start(f32[8,1,256]{2,1,0:T(1,128)} %broadcast_in_dim.12), calls=%async_computation | async-start | bytes 16384 | tf_op jit(solution)/shard_map/all_to_all | solution.py:16
  63.0 118.4 %all-to-all-start.1 = ((bf16[8,256,576]{1,2,0:T(8,128)(2,1)}), bf16[8,256,576]{1,2,0:T(8,128)(2,1)S(1)}, u32[]{:S(2)}, u32[]{:S(2)}) async-start(bf16[8,256,576]{1,2,0:T(8,128)(2,1)} %broadcast_in_dim.13), calls=%async_computation.1 | async-start | bytes 4718592 | tf_op jit(solution)/shard_map/all_to_all | solution.py:16
  181.4 4.6 %copy-start.1 = (bf16[8,256,576]{1,2,0:T(8,128)(2,1)}, bf16[8,256,576]{1,2,0:T(8,128)(2,1)S(1)}, u32[]{:S(2)}) copy-start(bf16[8,256,576]{1,2,0:T(8,128)(2,1)S(1)} %all-to-all-done.1) | copy-start | bytes 7077892
  193.9 1.7 copy-start.2
  362.3 5.3 %copy-start.3 = (bf16[576]{0:T(1024)(128)(2,1)S(1)}, bf16[576]{0:T(1024)(128)(2,1)}, u32[]{:S(2)}) copy-start(bf16[576]{0:T(1024)(128)(2,1)} %param.13) | copy-start | bytes 3460
  362.3 10.1 %copy-start = (bf16[256,576]{0,1:T(8,128)(2,1)S(1)}, bf16[256,576]{0,1:T(8,128)(2,1)}, u32[]{:S(2)}) copy-start(bf16[256,576]{0,1:T(8,128)(2,1)} %param.7) | copy-start | bytes 884740
  363.3 9.0 %all-to-all-start.3 = ((f32[8,1,256]{2,1,0:T(1,128)}), f32[8,1,256]{2,1,0:T(1,128)S(1)}, u32[]{:S(2)}, u32[]{:S(2)}) async-start(f32[8,1,256]{2,1,0:T(1,128)} %broadcast_in_dim.16), calls=%async_computation.3 | async-start | bytes 16384 | tf_op jit(solution)/shard_map/all_to_all | solution.py:16
Sparse Core Ops, SparseCore 0:
  9.4 160.3 all-gather.2
  171.9 130.5 all-gather.4
where the time goes:
time: 381 us; the launch traced here: 380 us
  waiting for transfers between devices  216 us (57%)
  blocking collectives  53.6 us (14%)
  starting transfers between devices  53.2 us (14%)
  local copies, waits for them, and re-layouts  22.7 us (6%)
  matrix products  15.1 us (4%)
  between operations  13.6 us (4%)
  other arithmetic  6.51 us (2%)
    all_gather x1, waiting for transfers between devices, on_device(): lax.all_gather(w_out, 'fsdp', axis=1, tiled=True)  104 us
    all_gather x1, waiting for transfers between devices, side_by_side(): lax.all_gather(both, axis, axis=dim, tiled=True)  102 us
    all_to_all x1, blocking collectives, summed_on_arrival(): lax.all_to_all(in_blocks(array, dim, count), axis, 0, 0, tiled=True)  53.6 us
    all_to_all x3, starting transfers between devices, copy_for_each(): lax.all_to_all(jnp.broadcast_to(array[None], (count, *array.shape)), axis...  53.1 us
    dot_general x4, local copies, waits for them, and re-layouts, on_device(): jnp.dot(whole, piece, preferred_element_type=jnp.float32)  16 us
    dot_general x3, matrix products, on_device(): jnp.dot(whole, piece, preferred_element_type=jnp.float32)  10.5 us
    all_to_all x3, waiting for transfers between devices, copy_for_each(): lax.all_to_all(jnp.broadcast_to(array[None], (count, *array.shape)), axis...  8.7 us
  transfers between devices with their start and end apart: 5, of which 4 were waited for; matrix products, arithmetic and copies ran while one was open for 9% of the time, Pallas kernels for 0%

commit v1 on v0

--- a/solution.py
+++ b/solution.py
@@ -9,6 +9,11 @@
 soft_cap = 50.0
 attn_scale = 144.0 ** (-0.5)
 rope_base = 10000.0
+
+
+def tiled_gather(x, axis, dim):
+    copies = jnp.concatenate([x] * lax.axis_size(axis), axis=dim)
+    return lax.all_to_all(copies, axis, dim, dim, tiled=True)
 
 
 def copy_for_each(array, axis):
@@ -101,7 +106,7 @@
     value = value_raw.astype(jnp.bfloat16).reshape(rows, local_kv, HEAD_DIM)
     attn = attend(query, key, value, position)
     partial_value = jnp.dot(
-        attn, lax.all_gather(w_out, "fsdp", axis=1, tiled=True), preferred_element_type=jnp.float32
+        attn, tiled_gather(w_out, "fsdp", 1), preferred_element_type=jnp.float32
     )
     proj = summed_on_arrival(partial_value.astype(jnp.bfloat16), "tensor", 1)
     post_total = of_everyone(jnp.sum(proj * proj, axis=1), "tensor")

time: 381 us -> 727 us (1.91)
  waiting for transfers between devices: 216 us -> 534 us
  local copies, waits for them, and re-layouts: 22.7 us -> 55.8 us
  blocking collectives: 53.6 us -> 42.4 us
  starting transfers between devices: 53.2 us -> 60.8 us
    all_gather x1, waiting for transfers between devices: 102 us -> 512 us  [side_by_side(): lax.all_gather(both, axis, axis=dim, tiled=True)]
    all_gather x1 -> x0, waiting for transfers between devices: 104 us -> none  [on_device(): lax.all_gather(w_out, 'fsdp', axis=1, tiled=True)]
    unnamed x8 -> x47, local copies, waits for them, and re-layouts: 1.07 us -> 33.6 us
    all_to_all x3, waiting for transfers between devices: 8.7 us -> 21.6 us  [copy_for_each(): lax.all_to_all(jnp.broadcast_to(array[None], (count, *array.shape)), axis...]
    all_to_all x1, blocking collectives: 53.6 us -> 42.4 us  [summed_on_arrival(): lax.all_to_all(in_blocks(array, dim, count), axis, 0, 0, tiled=True)]
  transfers between devices with their start and end apart: 5 -> 5, of which waited for: 4 -> 3; matrix products, arithmetic and copies ran while one was open for 9% -> 9% of each run, Pallas kernels for 0% -> 0%
where the time goes in v1:
time: 727 us; the launch traced here: 726 us
  waiting for transfers between devices  534 us (73%)
  starting transfers between devices  60.8 us (8%)
  local copies, waits for them, and re-layouts  55.8 us (8%)
  blocking collectives  42.4 us (6%)
  matrix products  14.4 us (2%)
  between operations  13.6 us (2%)
    all_gather x1, waiting for transfers between devices, side_by_side(): lax.all_gather(both, axis, axis=dim, tiled=True)  512 us
    all_to_all x3, starting transfers between devices, copy_for_each(): lax.all_to_all(jnp.broadcast_to(array[None], (count, *array.shape)), axis...  53.8 us
    all_to_all x1, blocking collectives, summed_on_arrival(): lax.all_to_all(in_blocks(array, dim, count), axis, 0, 0, tiled=True)  42.4 us
    unnamed x47, local copies, waits for them, and re-layouts  33.6 us
    all_to_all x3, waiting for transfers between devices, copy_for_each(): lax.all_to_all(jnp.broadcast_to(array[None], (count, *array.shape)), axis...  21.6 us
    dot_general x4, local copies, waits for them, and re-layouts, on_device(): jnp.dot(whole, piece, preferred_element_type=jnp.float32)  16 us
  transfers between devices with their start and end apart: 5, of which 3 were waited for; matrix products, arithmetic and copies ran while one was open for 9% of the time, Pallas kernels for 0%

profile of v1, /device:TPU:33, one launch (start us, length us, event | category | flops | bytes accessed | tf_op | source)
XLA Modules:
  0.0 726.2 jit_solution(4757934049023381167)
XLA Ops:
  6.5 1.1 fusion.10
  8.2 44.7 %all-to-all-start = ((f32[8,1,256]{2,1,0:T(1,128)}), f32[8,1,256]{2,1,0:T(1,128)S(1)}, u32[]{:S(2)}, u32[]{:S(2)}) async-start(f32[8,1,256]{2,1,0:T(1,128)} %broadcast_in_dim.12), calls=%async_computation | async-start | bytes 16384 | tf_op jit(solution)/shard_map/all_to_all | solution.py:21
  52.9 1.6 constant_dynamic-update-slice_fusion.31
  54.5 1.6 constant_dynamic-update-slice_fusion.30
  56.1 1.6 constant_dynamic-update-slice_fusion.29
  57.6 1.6 constant_dynamic-update-slice_fusion.28
  59.2 1.6 constant_dynamic-update-slice_fusion.27
  60.8 1.6 constant_dynamic-update-slice_fusion.26
  62.4 1.6 constant_dynamic-update-slice_fusion.25
  64.0 1.6 constant_dynamic-update-slice_fusion.24
  65.5 1.6 constant_dynamic-update-slice_fusion.23
  67.1 1.7 constant_dynamic-update-slice_fusion.22
  68.8 1.6 constant_dynamic-update-slice_fusion.21
  70.4 1.6 constant_dynamic-update-slice_fusion.20
  72.0 1.6 constant_dynamic-update-slice_fusion.19
  73.5 1.6 constant_dynamic-update-slice_fusion.18
  75.1 0.7 convert_element_type.60
  75.8 1.1 fusion.12
  77.0 1.6 broadcast_in_dim.13
  78.5 4.9 all-to-all-start.1
  84.1 0.7 constant_dynamic-update-slice_fusion.16
  85.4 0.7 constant_dynamic-update-slice_fusion.14
  86.1 0.7 constant_dynamic-update-slice_fusion.13
  86.7 0.7 constant_dynamic-update-slice_fusion.12
  87.4 0.7 constant_dynamic-update-slice_fusion.11
  88.1 0.7 constant_dynamic-update-slice_fusion.10
  88.8 0.7 constant_dynamic-update-slice_fusion.9
  90.1 0.7 constant_dynamic-update-slice_fusion.7
  91.4 0.7 constant_dynamic-update-slice_fusion.5
  92.1 0.7 constant_dynamic-update-slice_fusion.4
  92.8 0.7 constant_dynamic-update-slice_fusion.3
  95.5 16.9 %all-to-all-done.1 = bf16[8,256,576]{1,2,0:T(8,128)(2,1)S(1)} async-done(((bf16[8,256,576]{1,2,0:T(8,128)(2,1)}), bf16[8,256,576]{1,2,0:T(8,128)(2,1)S(1)}, u32[]{:S(2)}, u32[]{:S(2)}) %all-to-all-start.1) | async-done | bytes 2359328 | tf_op jit(solution)/shard_map/all_to_all | solution.py:21
  112.4 6.9 all-to-all-start.2
  119.4 0.7 pad_maximum_fusion
  120.6 511.9 %all-gather.2.cloned.1.call-done = bf16[4608,1024]{1,0:T(8,128)(2,1)} async-done(((bf16[144,1024]{1,0:T(8,128)(2,1)}), bf16[4608,1024]{1,0:T(8,128)(2,1)}) %all-gather.2.cloned.1.call-update) | async-done | bytes 9437200 | tf_op jit(solution)/shard_map/all_gather | solution.py:46
  632.5 4.7 slice_bitcast_fusion
  637.3 6.8 copy.36
  644.1 3.7 fusion.22
  648.2 1.8 slice_bitcast_fusion.1
  650.1 2.6 copy.34
  652.7 3.3 fusion.21
  656.6 2.8 fusion.7
  659.7 3.8 convolution_convert_fusion
  663.5 2.5 copy.42
  666.0 42.4 %all_to_all.34 = bf16[8,256,576]{1,2,0:T(8,128)(2,1)S(1)} all-to-all(bf16[8,256,576]{1,2,0:T(8,128)(2,1)} %bitcast.45), channel_id=1, replica_groups=mesh['groups'=2,'fsdp'=32,'tensor'=8] {'tensor'}, dimensions={0} | all-to-all | bytes 4718592 | tf_op jit(solution)/shard_map/all_to_all | solution.py:56
  709.4 4.3 all-to-all-start.4
  713.7 4.7 all-to-all-done.4
  718.4 1.0 convert_add_fusion
  (46 shorter events, 8.2 us)
Async XLA Ops:
  8.2 67.6 %all-to-all-start = ((f32[8,1,256]{2,1,0:T(1,128)}), f32[8,1,256]{2,1,0:T(1,128)S(1)}, u32[]{:S(2)}, u32[]{:S(2)}) async-start(f32[8,1,256]{2,1,0:T(1,128)} %broadcast_in_dim.12), calls=%async_computation | async-start | bytes 16384 | tf_op jit(solution)/shard_map/all_to_all | solution.py:21
  67.1 16.3 %copy-start = (bf16[512,144]{0,1:T(8,128)(2,1)S(1)}, bf16[512,144]{0,1:T(8,128)(2,1)}, u32[]{:S(2)}) copy-start(bf16[512,144]{0,1:T(8,128)(2,1)} %param.12) | copy-start | bytes 442372
  78.5 33.9 %all-to-all-start.1 = ((bf16[8,256,576]{1,2,0:T(8,128)(2,1)}), bf16[8,256,576]{1,2,0:T(8,128)(2,1)S(1)}, u32[]{:S(2)}, u32[]{:S(2)}) async-start(bf16[8,256,576]{1,2,0:T(8,128)(2,1)} %broadcast_in_dim.13), calls=%async_computation.1 | async-start | bytes 4718592 | tf_op jit(solution)/shard_map/all_to_all | solution.py:21
  112.4 531.6 %copy-start.2 = (bf16[8,256,576]{1,2,0:T(8,128)(2,1)}, bf16[8,256,576]{1,2,0:T(8,128)(2,1)S(1)}, u32[]{:S(2)}) copy-start(bf16[8,256,576]{1,2,0:T(8,128)(2,1)S(1)} %all-to-all-done.1) | copy-start | bytes 7077892
  112.4 7.0 copy-start.4
  112.4 7.0 copy-start.5
  112.4 7.0 copy-start.6
  112.4 547.3 %all-to-all-start.2 = ((bf16[512,32,144]{0,2,1:T(8,128)(2,1)}), bf16[512,32,144]{0,2,1:T(8,128)(2,1)}, u32[]{:S(2)}, u32[]{:S(2)}) async-start(bf16[512,32,144]{0,2,1:T(8,128)(2,1)} %bitcast.18), calls=%async_computation.2 | async-start | bytes 9437184 | tf_op jit(solution)/shard_map/all_to_all | solution.py:16
  119.3 513.2 %all-gather.2.cloned.1.call-start = ((), (), s32[]{:S(2)}) async-start(), calls=%async_computation.5 | async-start | bytes 9732096 | tf_op jit(solution)/shard_map/all_gather | solution.py:46
  652.7 3.9 copy-start.3
  666.0 47.7 %copy-start.7 = (bf16[576]{0:T(1024)(128)(2,1)S(1)}, bf16[576]{0:T(1024)(128)(2,1)}, u32[]{:S(2)}) copy-start(bf16[576]{0:T(1024)(128)(2,1)} %param.13) | copy-start | bytes 3460
  666.0 52.4 %copy-start.1 = (bf16[256,576]{0,1:T(8,128)(2,1)S(1)}, bf16[256,576]{0,1:T(8,128)(2,1)}, u32[]{:S(2)}) copy-start(bf16[256,576]{0,1:T(8,128)(2,1)} %param.7) | copy-start | bytes 884740
  709.4 9.0 %all-to-all-start.4 = ((f32[8,1,256]{2,1,0:T(1,128)}), f32[8,1,256]{2,1,0:T(1,128)S(1)}, u32[]{:S(2)}, u32[]{:S(2)}) async-start(f32[8,1,256]{2,1,0:T(1,128)} %broadcast_in_dim.16), calls=%async_computation.4 | async-start | bytes 16384 | tf_op jit(solution)/shard_map/all_to_all | solution.py:21
Sparse Core Ops, SparseCore 0:
  122.3 510.2 all-gather.1
